TPU v7x, 32 devices: a whole 2x2x4 slice. The times are simulated.
32 devices in a mesh: row: 4 (over y, x), col: 8 (over z, core).
Axes of the slice: x: 2, y: 2, z: 4, core: 2. Of those that a mesh axis runs over, the one named last changes fastest.
Arguments:
- left_matrix: float32 [4096, 4096], P('row', 'col'), may hold values from -6 to 6
- right_matrix: float32 [4096, 4096], P('row', 'col'), may hold values from -0.09375 to 0.09375
Outputs:
- product_matrix: float32 [4096, 4096], P('row', 'col')
All inputs are finite; a program needn't handle non-finite values.
Results may differ from a plain program's by a relative error of at most 0.00019.
Values sent between devices are 32-bit elements; how exact they have to be, the bound alone decides.
A program may use at most 64 MiB of HBM per device.

v0:
```python
import jax
import jax.numpy as jnp
from jax import lax
from jax.sharding import PartitionSpec as P


def multiply(left_term, right_term):
    return jnp.dot(
        left_term, right_term, precision=lax.Precision.HIGHEST, preferred_element_type=jnp.float32
    )


def body(left_matrix, right_matrix):
    row_panel = lax.all_gather(left_matrix, "col", axis=1, tiled=True)
    col_panel = lax.all_gather(right_matrix, "row", axis=0, tiled=True)
    return multiply(row_panel, col_panel)


def solution(mesh):
    placed = (P("row", "col"), P("row", "col"))
    return jax.shard_map(
        body, mesh=mesh, in_specs=placed, out_specs=P("row", "col"), check_vma=False
    )
```

profile of v0, /device:TPU:0, one launch (start us, length us, event | category | flops | bytes accessed | tf_op | source)
XLA Modules:
  0.0 289.9 jit_solution(7672909341723281923)
XLA Ops:
  6.5 0.0 all-gather.5.cloned.1.call-start
  6.5 0.7 all-gather.5.cloned.1.call-update
  7.3 0.0 all-gather.3.cloned.1.call-start
  7.3 0.7 all-gather.3.cloned.1.call-update
  8.0 91.4 %all-gather.5.cloned.1.call-done = f32[4096,512]{1,0:T(8,128)} async-done(((f32[1024,512]{1,0:T(8,128)}), f32[4096,512]{1,0:T(8,128)}) %all-gather.5.cloned.1.call-update) | async-done | bytes 8388624 | tf_op jit(solution)/shard_map/all_gather | solution.py:15
  99.4 152.7 %all-gather.3.cloned.1.call-done = f32[1024,4096]{1,0:T(8,128)} async-done(((f32[1024,512]{1,0:T(8,128)}), f32[1024,4096]{1,0:T(8,128)}) %all-gather.3.cloned.1.call-update) | async-done | bytes 16777232 | tf_op jit(solution)/shard_map/all_gather | solution.py:14
  252.1 31.0 %fusion = f32[1024,512]{1,0:T(8,128)} fusion(f32[1024,4096]{1,0:T(8,128)} %all-gather.3.cloned.1.call-done, f32[4096,512]{1,0:T(8,128)} %all-gather.5.cloned.1.call-done), kind=kOutput, calls=%fused_computation | convolution fusion | flops 25769803776 | bytes 27262976 | tf_op jit(solution)/shard_map/dot_general | solution.py:8
Async XLA Ops:
  6.5 92.9 %all-gather.5.cloned.1.call-start = ((), (), s32[]{:S(2)}) async-start(), calls=%async_computation.1 | async-start | bytes 10485760 | tf_op jit(solution)/shard_map/all_gather | solution.py:15
  7.3 244.9 %all-gather.3.cloned.1.call-start = ((), (), s32[]{:S(2)}) async-start(), calls=%async_computation | async-start | bytes 18874368 | tf_op jit(solution)/shard_map/all_gather | solution.py:14
Sparse Core Ops, SparseCore 0:
  9.2 90.1 all-gather.4
  101.0 151.0 all-gather.2
where the time goes:
time: 290 us
  waiting for transfers between devices  246 us (85%)
  matrix products  31 us (11%)
  between operations  13.4 us (5%)
    all_gather x1, waiting for transfers between devices, body(): row_panel = lax.all_gather(left_matrix, 'col', axis=1, tiled=True)  153 us
    all_gather x1, waiting for transfers between devices, body(): col_panel = lax.all_gather(right_matrix, 'row', axis=0, tiled=True)  91.4 us
    dot_general x1, matrix products, multiply(): jnp.dot(left_term, right_term, precision=lax.Precision.HIGHEST, preferred...  31 us
  transfers between devices with their start and end apart: 2, of which 2 were waited for; matrix products, arithmetic and copies ran while one was open for 0% of the time, Pallas kernels for 0%

commit v1 on v0

--- a/solution.py
+++ b/solution.py
@@ -11,7 +11,14 @@
 
 
 def body(left_matrix, right_matrix):
-    row_panel = lax.all_gather(left_matrix, "col", axis=1, tiled=True)
+    n_dev = lax.axis_size("col")
+    right = [(i, (i + 1) % n_dev) for i in range(n_dev)]
+    parts = [left_matrix]
+    for hop in range(1, n_dev):
+        parts = [lax.ppermute(parts[0], "col", right), *parts]
+    whole = jnp.concatenate(parts, axis=1)
+    shift = (lax.axis_index("col") + 1) * parts[-1].shape[1]
+    row_panel = jnp.roll(whole, shift, axis=1)
     col_panel = lax.all_gather(right_matrix, "row", axis=0, tiled=True)
     return multiply(row_panel, col_panel)
 

time: 290 us -> 285 us (0.983)
  waiting for transfers between devices: 246 us -> 193 us
  local copies, waits for them, and re-layouts: 0 us -> 46.6 us
    ppermute x0 -> x7, waiting for transfers between devices: none -> 193 us  [body(): parts = [lax.ppermute(parts[0], 'col', right), *parts]]
    all_gather x1 -> x0, waiting for transfers between devices: 153 us -> none  [body(): row_panel = lax.all_gather(left_matrix, 'col', axis=1, tiled=True)]
    all_gather x1, waiting for transfers between devices: 91.4 us -> 0.01 us  [body(): col_panel = lax.all_gather(right_matrix, 'row', axis=0, tiled=True)]
    unnamed x0 -> x29, local copies, waits for them, and re-layouts: none -> 45.1 us
  transfers between devices with their start and end apart: 2 -> 8, of which waited for: 2 -> 7; matrix products, arithmetic and copies ran while one was open for 0% -> 15% of each run, Pallas kernels for 0% -> 0%
where the time goes in v1:
time: 285 us; the launch traced here: 284 us
  waiting for transfers between devices  193 us (68%)
  local copies, waits for them, and re-layouts  46.6 us (16%)
  matrix products  31 us (11%)
  between operations  13.4 us (5%)
    ppermute x7, waiting for transfers between devices, body(): parts = [lax.ppermute(parts[0], 'col', right), *parts]  193 us
    unnamed x29, local copies, waits for them, and re-layouts  45.1 us
    dot_general x1, matrix products, multiply(): jnp.dot(left_term, right_term, precision=lax.Precision.HIGHEST, preferred...  31 us
  transfers between devices with their start and end apart: 8, of which 7 were waited for; matrix products, arithmetic and copies ran while one was open for 15% of the time, Pallas kernels for 0%

profile of v1, /device:TPU:0, one launch (start us, length us, event | category | flops | bytes accessed | tf_op | source)
XLA Modules:
  0.0 284.1 jit_solution(11674482978669563647)
XLA Ops:
  6.5 0.0 copy-start
  6.5 0.0 all-gather.2.cloned.1.call-start
  6.5 0.5 collective-permute-start
  7.0 28.0 %collective-permute-done = f32[1024,512]{1,0:T(8,128)S(1)} collective-permute-done((f32[1024,512]{1,0:T(8,128)}, f32[1024,512]{1,0:T(8,128)S(1)}, u32[]{:S(2)}, u32[]{:S(2)}) %collective-permute-start) | collective-permute-done | bytes 2097184 | tf_op jit(solution)/shard_map/ppermute | solution.py:18
  35.1 0.0 copy-start.1
  35.1 1.4 copy-done.1
  36.4 0.0 collective-permute-start.1
  36.4 27.4 %collective-permute-done.1 = f32[1024,512]{1,0:T(8,128)} collective-permute-done((f32[1024,512]{1,0:T(8,128)S(1)}, f32[1024,512]{1,0:T(8,128)}, u32[]{:S(2)}, u32[]{:S(2)}) %collective-permute-start.1) | collective-permute-done | bytes 2097184 | tf_op jit(solution)/shard_map/ppermute | solution.py:18
  63.8 0.0 collective-permute-start.2
  63.8 0.0 all-gather.2.cloned.1.call-update
  63.8 27.5 %collective-permute-done.2 = f32[1024,512]{1,0:T(8,128)} collective-permute-done((f32[1024,512]{1,0:T(8,128)}, f32[1024,512]{1,0:T(8,128)}, u32[]{:S(2)}, u32[]{:S(2)}) %collective-permute-start.2) | collective-permute-done | bytes 2097184 | tf_op jit(solution)/shard_map/ppermute | solution.py:18
  91.4 0.0 collective-permute-start.3
  91.4 27.5 %collective-permute-done.3 = f32[1024,512]{1,0:T(8,128)S(1)} collective-permute-done((f32[1024,512]{1,0:T(8,128)}, f32[1024,512]{1,0:T(8,128)S(1)}, u32[]{:S(2)}, u32[]{:S(2)}) %collective-permute-start.3) | collective-permute-done | bytes 2097184 | tf_op jit(solution)/shard_map/ppermute | solution.py:18
  118.8 0.0 copy-start.3
  118.8 1.3 copy-done.3
  120.2 0.0 collective-permute-start.4
  120.2 27.3 %collective-permute-done.4 = f32[1024,512]{1,0:T(8,128)S(1)} collective-permute-done((f32[1024,512]{1,0:T(8,128)S(1)}, f32[1024,512]{1,0:T(8,128)S(1)}, u32[]{:S(2)}, u32[]{:S(2)}) %collective-permute-start.4) | collective-permute-done | bytes 2097184 | tf_op jit(solution)/shard_map/ppermute | solution.py:18
  147.4 0.0 copy-start.5
  147.4 1.3 copy-done.5
  148.7 0.0 collective-permute-start.5
  148.7 27.4 %collective-permute-done.5 = f32[1024,512]{1,0:T(8,128)} collective-permute-done((f32[1024,512]{1,0:T(8,128)S(1)}, f32[1024,512]{1,0:T(8,128)}, u32[]{:S(2)}, u32[]{:S(2)}) %collective-permute-start.5) | collective-permute-done | bytes 2097184 | tf_op jit(solution)/shard_map/ppermute | solution.py:18
  176.1 0.0 collective-permute-start.6
  176.1 0.0 copy-start.6
  176.1 0.0 copy-start.4
  176.1 0.0 copy-start.2
  176.1 27.6 %collective-permute-done.6 = f32[1024,512]{1,0:T(8,128)} collective-permute-done((f32[1024,512]{1,0:T(8,128)}, f32[1024,512]{1,0:T(8,128)}, u32[]{:S(2)}, u32[]{:S(2)}) %collective-permute-start.6) | collective-permute-done | bytes 2097184 | tf_op jit(solution)/shard_map/ppermute | solution.py:18
  203.7 3.1 %constant_dynamic-update-slice_fusion.15 = f32[1024,8192]{1,0:T(8,128)} fusion(f32[1024,512]{1,0:T(8,128)} %collective-permute-done.6), kind=kLoop, calls=%fused_computation.17 | loop fusion | bytes 4194304
  206.7 3.0 %constant_dynamic-update-slice_fusion.14 = f32[1024,8192]{1,0:T(8,128)} fusion(f32[1024,8192]{1,0:T(8,128)} %constant_dynamic-update-slice_fusion.15, f32[1024,512]{1,0:T(8,128)} %collective-permute-done.5), kind=kLoop, calls=%fused_computation.16 | loop fusion | bytes 4194304
  209.8 3.1 %constant_dynamic-update-slice_fusion.13 = f32[1024,8192]{1,0:T(8,128)} fusion(f32[1024,8192]{1,0:T(8,128)} %constant_dynamic-update-slice_fusion.14, f32[1024,512]{1,0:T(8,128)} %copy-done.5), kind=kLoop, calls=%fused_computation.15 | loop fusion | bytes 4194304
  212.8 3.0 %constant_dynamic-update-slice_fusion.12 = f32[1024,8192]{1,0:T(8,128)} fusion(f32[1024,8192]{1,0:T(8,128)} %constant_dynamic-update-slice_fusion.13, f32[1024,512]{1,0:T(8,128)} %copy-done.3), kind=kLoop, calls=%fused_computation.14 | loop fusion | bytes 4194304
  215.9 3.0 %constant_dynamic-update-slice_fusion.11 = f32[1024,8192]{1,0:T(8,128)} fusion(f32[1024,8192]{1,0:T(8,128)} %constant_dynamic-update-slice_fusion.12, f32[1024,512]{1,0:T(8,128)} %collective-permute-done.2), kind=kLoop, calls=%fused_computation.13 | loop fusion | bytes 4194304
  218.9 3.1 %constant_dynamic-update-slice_fusion.10 = f32[1024,8192]{1,0:T(8,128)} fusion(f32[1024,8192]{1,0:T(8,128)} %constant_dynamic-update-slice_fusion.11, f32[1024,512]{1,0:T(8,128)} %collective-permute-done.1), kind=kLoop, calls=%fused_computation.12 | loop fusion | bytes 4194304
  222.0 3.1 %constant_dynamic-update-slice_fusion.9 = f32[1024,8192]{1,0:T(8,128)} fusion(f32[1024,8192]{1,0:T(8,128)} %constant_dynamic-update-slice_fusion.10, f32[1024,512]{1,0:T(8,128)} %copy-done.1), kind=kLoop, calls=%fused_computation.11 | loop fusion | bytes 4194304
  225.0 3.1 %constant_dynamic-update-slice_fusion.8 = f32[1024,8192]{1,0:T(8,128)} fusion(f32[1024,8192]{1,0:T(8,128)} %constant_dynamic-update-slice_fusion.9, f32[1024,512]{1,0:T(8,128)} %param.2), kind=kLoop, calls=%fused_computation.10 | loop fusion | bytes 4194304
  228.1 3.1 %constant_dynamic-update-slice_fusion.7 = f32[1024,8192]{1,0:T(8,128)} fusion(f32[1024,8192]{1,0:T(8,128)} %constant_dynamic-update-slice_fusion.8, f32[1024,512]{1,0:T(8,128)} %collective-permute-done.6), kind=kLoop, calls=%fused_computation.9 | loop fusion | bytes 4194304
  231.2 3.1 %constant_dynamic-update-slice_fusion.6 = f32[1024,8192]{1,0:T(8,128)} fusion(f32[1024,8192]{1,0:T(8,128)} %constant_dynamic-update-slice_fusion.7, f32[1024,512]{1,0:T(8,128)} %collective-permute-done.5), kind=kLoop, calls=%fused_computation.8 | loop fusion | bytes 4194304
  234.2 0.0 copy-done.6
  234.2 1.5 constant_dynamic-update-slice_fusion.5
  235.7 0.0 copy-done.4
  235.7 1.5 constant_dynamic-update-slice_fusion.4
  237.2 3.1 %constant_dynamic-update-slice_fusion.3 = f32[1024,8192]{1,0:T(8,128)} fusion(f32[1024,8192]{1,0:T(8,128)} %constant_dynamic-update-slice_fusion.4, f32[1024,512]{1,0:T(8,128)} %collective-permute-done.2), kind=kLoop, calls=%fused_computation.5 | loop fusion | bytes 4194304
  240.2 3.1 %constant_dynamic-update-slice_fusion.2 = f32[1024,8192]{1,0:T(8,128)} fusion(f32[1024,8192]{1,0:T(8,128)} %constant_dynamic-update-slice_fusion.3, f32[1024,512]{1,0:T(8,128)} %collective-permute-done.1), kind=kLoop, calls=%fused_computation.4 | loop fusion | bytes 4194304
  243.3 0.0 copy-done.2
  243.3 1.5 constant_dynamic-update-slice_fusion.1
  244.8 0.0 copy-done
  244.8 1.5 constant_dynamic-update-slice_fusion
  246.3 0.0 all-gather.2.cloned.1.call-done
  246.3 31.0 %fusion = f32[1024,512]{1,0:T(8,128)} fusion(f32[4096,512]{1,0:T(8,128)} %all-gather.2.cloned.1.call-done, f32[1024,8192]{1,0:T(8,128)} %constant_dynamic-update-slice_fusion, s32[]{:T(128)S(6)} %select_n.14), kind=kOutput, calls=%fused_computation | convolution fusion | flops 25769803776 | bytes 27262980 | tf_op jit(solution)/shard_map/dot_general | solution.py:8
Async XLA Ops:
  6.5 238.3 %copy-start = (f32[1024,512]{1,0:T(8,128)S(1)}, f32[1024,512]{1,0:T(8,128)}, u32[]{:S(2)}) copy-start(f32[1024,512]{1,0:T(8,128)} %param.2) | copy-start | bytes 6291460
  6.5 239.7 %all-gather.2.cloned.1.call-start = ((), (), s32[]{:S(2)}) async-start(), calls=%async_computation | async-start | bytes 10485760 | tf_op jit(solution)/shard_map/all_gather | solution.py:22
  6.5 28.5 %collective-permute-start = (f32[1024,512]{1,0:T(8,128)}, f32[1024,512]{1,0:T(8,128)S(1)}, u32[]{:S(2)}, u32[]{:S(2)}) collective-permute-start(f32[1024,512]{1,0:T(8,128)} %param.2), channel_id=1, source_target_pairs={{0,1},{1,2},{2,3},{3,4},{4,5},{5,6},{6,7},{7,0},{8,9},{9,10},{10,1... | collective-permute-start | bytes 6291464 | tf_op jit(solution)/shard_map/ppermute | solution.py:18
  35.1 1.4 copy-start.1
  36.4 27.4 %collective-permute-start.1 = (f32[1024,512]{1,0:T(8,128)S(1)}, f32[1024,512]{1,0:T(8,128)}, u32[]{:S(2)}, u32[]{:S(2)}) collective-permute-start(f32[1024,512]{1,0:T(8,128)S(1)} %collective-permute-done), channel_id=1, source_target_pairs={{0,1},{1,2},{2,3},{3,4},{4,5},{5,6},{6,7},{7,0},{8,9},{9,10},{10,1... | collective-permute-start | bytes 6291464 | tf_op jit(solution)/shard_map/ppermute | solution.py:18
  63.8 27.6 %collective-permute-start.2 = (f32[1024,512]{1,0:T(8,128)}, f32[1024,512]{1,0:T(8,128)}, u32[]{:S(2)}, u32[]{:S(2)}) collective-permute-start(f32[1024,512]{1,0:T(8,128)} %collective-permute-done.1), channel_id=1, source_target_pairs={{0,1},{1,2},{2,3},{3,4},{4,5},{5,6},{6,7},{7,0},{8,9},{9,10},{10,1... | collective-permute-start | bytes 6291464 | tf_op jit(solution)/shard_map/ppermute | solution.py:18
  91.4 27.5 %collective-permute-start.3 = (f32[1024,512]{1,0:T(8,128)}, f32[1024,512]{1,0:T(8,128)S(1)}, u32[]{:S(2)}, u32[]{:S(2)}) collective-permute-start(f32[1024,512]{1,0:T(8,128)} %collective-permute-done.2), channel_id=1, source_target_pairs={{0,1},{1,2},{2,3},{3,4},{4,5},{5,6},{6,7},{7,0},{8,9},{9,10},{10,1... | collective-permute-start | bytes 6291464 | tf_op jit(solution)/shard_map/ppermute | solution.py:18
  118.8 1.3 copy-start.3
  120.2 27.3 %collective-permute-start.4 = (f32[1024,512]{1,0:T(8,128)S(1)}, f32[1024,512]{1,0:T(8,128)S(1)}, u32[]{:S(2)}, u32[]{:S(2)}) collective-permute-start(f32[1024,512]{1,0:T(8,128)S(1)} %collective-permute-done.3), channel_id=1, source_target_pairs={{0,1},{1,2},{2,3},{3,4},{4,5},{5,6},{6,7},{7,0},{8,9},{9,10},{10,1... | collective-permute-start | bytes 6291464 | tf_op jit(solution)/shard_map/ppermute | solution.py:18
  147.4 1.3 copy-start.5
  148.7 27.4 %collective-permute-start.5 = (f32[1024,512]{1,0:T(8,128)S(1)}, f32[1024,512]{1,0:T(8,128)}, u32[]{:S(2)}, u32[]{:S(2)}) collective-permute-start(f32[1024,512]{1,0:T(8,128)S(1)} %collective-permute-done.4), channel_id=1, source_target_pairs={{0,1},{1,2},{2,3},{3,4},{4,5},{5,6},{6,7},{7,0},{8,9},{9,10},{10,1... | collective-permute-start | bytes 6291464 | tf_op jit(solution)/shard_map/ppermute | solution.py:18
  176.1 27.6 %collective-permute-start.6 = (f32[1024,512]{1,0:T(8,128)}, f32[1024,512]{1,0:T(8,128)}, u32[]{:S(2)}, u32[]{:S(2)}) collective-permute-start(f32[1024,512]{1,0:T(8,128)} %collective-permute-done.5), channel_id=1, source_target_pairs={{0,1},{1,2},{2,3},{3,4},{4,5},{5,6},{6,7},{7,0},{8,9},{9,10},{10,1... | collective-permute-start | bytes 6291464 | tf_op jit(solution)/shard_map/ppermute | solution.py:18
  176.1 58.1 %copy-start.6 = (f32[1024,512]{1,0:T(8,128)S(1)}, f32[1024,512]{1,0:T(8,128)}, u32[]{:S(2)}) copy-start(f32[1024,512]{1,0:T(8,128)} %copy-done.5) | copy-start | bytes 6291460
  176.1 59.6 %copy-start.4 = (f32[1024,512]{1,0:T(8,128)S(1)}, f32[1024,512]{1,0:T(8,128)}, u32[]{:S(2)}) copy-start(f32[1024,512]{1,0:T(8,128)} %copy-done.3) | copy-start | bytes 6291460
  176.1 67.2 %copy-start.2 = (f32[1024,512]{1,0:T(8,128)S(1)}, f32[1024,512]{1,0:T(8,128)}, u32[]{:S(2)}) copy-start(f32[1024,512]{1,0:T(8,128)} %copy-done.1) | copy-start | bytes 6291460
Sparse Core Ops, SparseCore 0:
  63.9 89.1 all-gather.1

commit v2 on v0

--- a/solution.py
+++ b/solution.py
@@ -12,7 +12,13 @@
 
 def body(left_matrix, right_matrix):
     row_panel = lax.all_gather(left_matrix, "col", axis=1, tiled=True)
-    col_panel = lax.all_gather(right_matrix, "row", axis=0, tiled=True)
+    count = lax.axis_size("row")
+    current, pieces = (right_matrix, [right_matrix])
+    for _ in range(count - 1):
+        current = lax.ppermute(current, "row", [(i, (i + 1) % count) for i in range(count)])
+        pieces.insert(0, current)
+    line = jnp.concatenate(pieces, axis=0)
+    col_panel = jnp.roll(line, (lax.axis_index("row") + 1) * right_matrix.shape[0], axis=0)
     return multiply(row_panel, col_panel)
 
 

time: 290 us -> 240 us (0.83)
  waiting for transfers between devices: 246 us -> 142 us
  local copies, waits for them, and re-layouts: 0 us -> 24.7 us
  matrix products: 31 us -> 55.6 us
  starting transfers between devices: 0.04 us -> 3.81 us
    all_gather x1, waiting for transfers between devices: 153 us -> 0.01 us  [body(): row_panel = lax.all_gather(left_matrix, 'col', axis=1, tiled=True)]
    ppermute x0 -> x3, waiting for transfers between devices: none -> 141 us  [body(): lax.ppermute(current, 'row', [(i, (i + 1) % count) for i in range(count)])]
    all_gather x1 -> x0, waiting for transfers between devices: 91.4 us -> none  [body(): col_panel = lax.all_gather(right_matrix, 'row', axis=0, tiled=True)]
    dot_general x1, matrix products: 31 us -> 55.6 us  [multiply(): jnp.dot(left_term, right_term, precision=lax.Precision.HIGHEST, preferred...]
    unnamed x0 -> x13, local copies, waits for them, and re-layouts: none -> 21.5 us
    ppermute x0 -> x3, starting transfers between devices: none -> 3.8 us  [body(): lax.ppermute(current, 'row', [(i, (i + 1) % count) for i in range(count)])]
  transfers between devices with their start and end apart: 2 -> 4, of which waited for: 2 -> 3; matrix products, arithmetic and copies ran while one was open for 0% -> 9% of each run, Pallas kernels for 0% -> 0%
where the time goes in v2:
time: 240 us; the launch traced here: 239 us
  waiting for transfers between devices  142 us (59%)
  matrix products  55.6 us (23%)
  local copies, waits for them, and re-layouts  24.7 us (10%)
  between operations  13.4 us (6%)
  starting transfers between devices  3.81 us (2%)
    ppermute x3, waiting for transfers between devices, body(): lax.ppermute(current, 'row', [(i, (i + 1) % count) for i in range(count)])  141 us
    dot_general x1, matrix products, multiply(): jnp.dot(left_term, right_term, precision=lax.Precision.HIGHEST, preferred...  55.6 us
    unnamed x13, local copies, waits for them, and re-layouts  21.5 us
  transfers between devices with their start and end apart: 4, of which 3 were waited for; matrix products, arithmetic and copies ran while one was open for 9% of the time, Pallas kernels for 0%

profile of v2, /device:TPU:0, one launch (start us, length us, event | category | flops | bytes accessed | tf_op | source)
XLA Modules:
  0.0 239.4 jit_solution(10999509172959733152)
XLA Ops:
  6.5 0.0 copy-start
  6.5 0.0 all-gather.2.cloned.1.call-start
  6.5 0.7 all-gather.2.cloned.1.call-update
  7.3 3.0 %collective-permute-start = (f32[1024,512]{1,0:T(8,128)}, f32[1024,512]{1,0:T(8,128)S(1)}, u32[]{:S(2)}, u32[]{:S(2)}) collective-permute-start(f32[1024,512]{1,0:T(8,128)} %param.3), channel_id=1, source_target_pairs={{0,8},{8,16},{16,24},{24,0},{1,9},{9,17},{17,25},{25,1},{2,10},{10... | collective-permute-start | bytes 6291464 | tf_op jit(solution)/shard_map/ppermute | solution.py:18
  10.3 46.8 %collective-permute-done = f32[1024,512]{1,0:T(8,128)S(1)} collective-permute-done((f32[1024,512]{1,0:T(8,128)}, f32[1024,512]{1,0:T(8,128)S(1)}, u32[]{:S(2)}, u32[]{:S(2)}) %collective-permute-start) | collective-permute-done | bytes 2097184 | tf_op jit(solution)/shard_map/ppermute | solution.py:18
  57.1 0.0 copy-start.1
  57.1 1.3 copy-done.1
  58.4 0.8 collective-permute-start.1
  59.2 47.1 %collective-permute-done.1 = f32[1024,512]{1,0:T(8,128)} collective-permute-done((f32[1024,512]{1,0:T(8,128)S(1)}, f32[1024,512]{1,0:T(8,128)}, u32[]{:S(2)}, u32[]{:S(2)}) %collective-permute-start.1) | collective-permute-done | bytes 2097184 | tf_op jit(solution)/shard_map/ppermute | solution.py:18
  106.3 0.0 collective-permute-start.2
  106.3 0.0 copy-start.2
  106.3 47.3 %collective-permute-done.2 = f32[1024,512]{1,0:T(8,128)} collective-permute-done((f32[1024,512]{1,0:T(8,128)}, f32[1024,512]{1,0:T(8,128)}, u32[]{:S(2)}, u32[]{:S(2)}) %collective-permute-start.2) | collective-permute-done | bytes 2097184 | tf_op jit(solution)/shard_map/ppermute | solution.py:18
  153.6 3.2 %constant_dynamic-update-slice_fusion.7 = f32[8192,512]{1,0:T(8,128)} fusion(f32[1024,512]{1,0:T(8,128)} %collective-permute-done.2), kind=kLoop, calls=%fused_computation.10 | loop fusion | bytes 4194304
  156.7 3.1 %constant_dynamic-update-slice_fusion.6 = f32[8192,512]{1,0:T(8,128)} fusion(f32[8192,512]{1,0:T(8,128)} %constant_dynamic-update-slice_fusion.7, f32[1024,512]{1,0:T(8,128)} %collective-permute-done.1), kind=kLoop, calls=%fused_computation.9 | loop fusion | bytes 4194304
  159.8 3.1 %constant_dynamic-update-slice_fusion.5 = f32[8192,512]{1,0:T(8,128)} fusion(f32[8192,512]{1,0:T(8,128)} %constant_dynamic-update-slice_fusion.6, f32[1024,512]{1,0:T(8,128)} %copy-done.1), kind=kLoop, calls=%fused_computation.8 | loop fusion | bytes 4194304
  162.9 3.1 %constant_dynamic-update-slice_fusion.4 = f32[8192,512]{1,0:T(8,128)} fusion(f32[8192,512]{1,0:T(8,128)} %constant_dynamic-update-slice_fusion.5, f32[1024,512]{1,0:T(8,128)} %param.3), kind=kLoop, calls=%fused_computation.7 | loop fusion | bytes 4194304
  166.0 3.1 %constant_dynamic-update-slice_fusion.3 = f32[8192,512]{1,0:T(8,128)} fusion(f32[8192,512]{1,0:T(8,128)} %constant_dynamic-update-slice_fusion.4, f32[1024,512]{1,0:T(8,128)} %collective-permute-done.2), kind=kLoop, calls=%fused_computation.6 | loop fusion | bytes 4194304
  169.1 3.1 %constant_dynamic-update-slice_fusion.2 = f32[8192,512]{1,0:T(8,128)} fusion(f32[8192,512]{1,0:T(8,128)} %constant_dynamic-update-slice_fusion.3, f32[1024,512]{1,0:T(8,128)} %collective-permute-done.1), kind=kLoop, calls=%fused_computation.5 | loop fusion | bytes 4194304
  172.2 0.0 copy-done.2
  172.2 1.5 constant_dynamic-update-slice_fusion.1
  173.7 0.0 copy-done
  173.7 1.5 constant_dynamic-update-slice_fusion
  175.2 0.0 all-gather.2.cloned.1.call-done
  175.2 55.6 %fusion.2 = f32[1024,512]{0,1:T(8,128)S(1)} fusion(f32[1024,4096]{1,0:T(8,128)} %all-gather.2.cloned.1.call-done, f32[8192,512]{1,0:T(8,128)} %constant_dynamic-update-slice_fusion, s32[]{:T(128)S(6)} %select_n.14), kind=kOutput, calls=%fused_computation.2 | convolution fusion | flops 25769803776 | bytes 27262980 | tf_op jit(solution)/shard_map/dot_general | solution.py:8
  230.8 1.8 copy.3
Async XLA Ops:
  6.5 167.2 %copy-start = (f32[1024,512]{1,0:T(8,128)S(1)}, f32[1024,512]{1,0:T(8,128)}, u32[]{:S(2)}) copy-start(f32[1024,512]{1,0:T(8,128)} %param.3) | copy-start | bytes 6291460
  6.5 168.6 %all-gather.2.cloned.1.call-start = ((), (), s32[]{:S(2)}) async-start(), calls=%async_computation | async-start | bytes 18874368 | tf_op jit(solution)/shard_map/all_gather | solution.py:14
  7.3 49.8 %collective-permute-start = (f32[1024,512]{1,0:T(8,128)}, f32[1024,512]{1,0:T(8,128)S(1)}, u32[]{:S(2)}, u32[]{:S(2)}) collective-permute-start(f32[1024,512]{1,0:T(8,128)} %param.3), channel_id=1, source_target_pairs={{0,8},{8,16},{16,24},{24,0},{1,9},{9,17},{17,25},{25,1},{2,10},{10... | collective-permute-start | bytes 6291464 | tf_op jit(solution)/shard_map/ppermute | solution.py:18
  57.1 1.3 copy-start.1
  58.4 47.9 %collective-permute-start.1 = (f32[1024,512]{1,0:T(8,128)S(1)}, f32[1024,512]{1,0:T(8,128)}, u32[]{:S(2)}, u32[]{:S(2)}) collective-permute-start(f32[1024,512]{1,0:T(8,128)S(1)} %collective-permute-done), channel_id=1, source_target_pairs={{0,8},{8,16},{16,24},{24,0},{1,9},{9,17},{17,25},{25,1},{2,10},{10... | collective-permute-start | bytes 6291464 | tf_op jit(solution)/shard_map/ppermute | solution.py:18
  106.3 47.3 %collective-permute-start.2 = (f32[1024,512]{1,0:T(8,128)}, f32[1024,512]{1,0:T(8,128)}, u32[]{:S(2)}, u32[]{:S(2)}) collective-permute-start(f32[1024,512]{1,0:T(8,128)} %collective-permute-done.1), channel_id=1, source_target_pairs={{0,8},{8,16},{16,24},{24,0},{1,9},{9,17},{17,25},{25,1},{2,10},{10... | collective-permute-start | bytes 6291464 | tf_op jit(solution)/shard_map/ppermute | solution.py:18
  106.3 65.9 %copy-start.2 = (f32[1024,512]{1,0:T(8,128)S(1)}, f32[1024,512]{1,0:T(8,128)}, u32[]{:S(2)}) copy-start(f32[1024,512]{1,0:T(8,128)} %copy-done.1) | copy-start | bytes 6291460
Sparse Core Ops, SparseCore 0:
  8.9 153.7 all-gather.1
